TPU v7x, 32 devices: a whole 2x2x4 slice. The times are simulated.
32 devices in a mesh: row: 8 (over z, core), col: 4 (over y, x).
Axes of the slice: x: 2, y: 2, z: 4, core: 2. Of those that a mesh axis runs over, the one named last changes fastest.
Arguments:
- hamiltonian: bfloat16 [36864, 36864], P('row', 'col'), may hold values from -0.6 to 0.6, as said below
- start_vectors: float32 [8, 4, 9216], P(None, 'col', 'row'), may hold values from -20 to 20
Outputs:
- last_vectors: float32 [8, 36864], P(None, ('row', 'col'))
- moments: float32 [8, 4], replicated
Inputs may be any that keep to these rules, and one draw needn't show every extreme that they name: `hamiltonian`: the matrix is exactly symmetric.
All inputs are finite; a program needn't handle non-finite values.
Results may differ from a plain program's by a relative error of at most 0.0024.
Values may be sent and summed in bfloat16 or wider, within the bound.
No kernel may reach another device: no remote copies, remote signals or barrier semaphores. Data moves between devices by JAX's collectives and lax.ppermute only.
A program may use at most 128 MiB of HBM per device.

v0:
```python
import jax
import jax.numpy as jnp
from jax import lax
from jax.sharding import PartitionSpec as P

STEPS = 3
ORDER = 36864


def reduce_cols(product):
    return lax.psum_scatter(product, "col", scatter_dimension=1, tiled=True)


def reduce_rows(product):
    return lax.psum_scatter(product, "row", scatter_dimension=1, tiled=True)


def from_columns(narrow, hamiltonian):
    vec_count = narrow.shape[0]

    def accumulate(running, portion, offset):
        return lax.dot_general(
            portion, hamiltonian, (((1,), (1,)), ((), ())), preferred_element_type=jnp.float32
        )

    empty = jnp.zeros((vec_count, hamiltonian.shape[0]), jnp.float32)
    return accumulate(empty, lax.all_gather(narrow, "row", axis=1, tiled=True), jnp.int32(0))


def from_rows(narrow, hamiltonian):
    vec_count = narrow.shape[0]

    def accumulate(running, portion, offset):
        return jnp.dot(portion, hamiltonian, preferred_element_type=jnp.float32)

    empty = jnp.zeros((vec_count, hamiltonian.shape[1]), jnp.float32)
    return accumulate(empty, lax.all_gather(narrow, "col", axis=1, tiled=True), jnp.int32(0))


def reduce_each(partial_sq):
    return lax.psum(partial_sq, ("row", "col"))


def per_device(hamiltonian, start_vectors):
    current = start_vectors[:, 0, :]
    partials = [jnp.sum(current * current, axis=1) / ORDER]
    previous = current
    for level in range(STEPS):
        narrow = current.astype(jnp.bfloat16)
        if level % 2 == 0:
            applied = reduce_cols(from_columns(narrow, hamiltonian))
        else:
            applied = reduce_rows(from_rows(narrow, hamiltonian))
        if level == 0:
            following = applied
        else:
            following = 2.0 * applied - previous
        previous = current
        current = following
        partials.append(jnp.sum(current * current, axis=1) / ORDER)
    squares = jnp.stack([reduce_each(partial_sq) for partial_sq in partials], axis=1)
    moments = jnp.concatenate([squares[:, :1], 2.0 * squares[:, 1:] - squares[:, :1]], axis=1)
    return (current, moments)


def solution(mesh):
    return jax.shard_map(
        per_device,
        mesh=mesh,
        in_specs=(P("row", "col"), P(None, "col", "row")),
        out_specs=(P(None, ("row", "col")), P()),
        check_vma=False,
    )
```

profile of v0, /device:TPU:0, one launch (start us, length us, event | category | flops | bytes accessed | tf_op | source)
XLA Modules:
  0.0 266.1 jit_solution(2623065425881969994)
XLA Ops:
  7.2 0.0 reduce-scatter.4.cloned.1.call-start
  7.2 0.8 copy.12
  8.0 15.7 %all_gather.9 = bf16[8,9216]{1,0:T(8,128)(2,1)S(1)} all-gather(bf16[8,1152]{1,0:T(8,128)(2,1)S(1)} %bitcast.24), channel_id=1, replica_groups=mesh['row'=8,'col'=4] {'row'}, dimensions={1}, use_global_device_ids=true | all-gather | bytes 165888 | tf_op jit(solution)/shard_map/all_gather | solution.py:27
  23.7 0.0 copy-start.1
  23.7 31.8 %fusion.3 = f32[8,4608]{1,0:T(8,128)} fusion(bf16[8,9216]{1,0:T(8,128)(2,1)S(1)} %all_gather.9, bf16[4608,9216]{1,0:T(8,128)(2,1)} %param.2), kind=kOutput, calls=%fused_computation.16 | convolution fusion | flops 679477248 | bytes 85229568 | tf_op jit(solution)/shard_map/dot_general | solution.py:22
  55.5 0.0 reduce-scatter.4.cloned.1.call-update
  55.5 0.0 reduce-scatter.6.cloned.1.call-start
  55.6 24.7 %reduce-scatter.4.cloned.1.call-done = f32[8,1152]{1,0:T(8,128)} async-done(((f32[8,4608]{1,0:T(8,128)}), f32[8,1152]{1,0:T(8,128)}) %reduce-scatter.4.cloned.1.call-update) | async-done | bytes 36880 | tf_op jit(solution)/shard_map/reduce_scatter | solution.py:11
  80.3 0.8 convert_element_type.10
  81.0 8.2 %all_gather.10 = bf16[8,4608]{1,0:T(8,128)(2,1)S(1)} all-gather(bf16[8,1152]{1,0:T(8,128)(2,1)S(1)} %convert_element_type.10), channel_id=1, replica_groups=mesh['row'=8,'col'=4] {'col'}, dimensions={1}, use_global_device_ids=true | all-gather | bytes 92160 | tf_op jit(solution)/shard_map/all_gather | solution.py:37
  89.3 0.0 copy-start
  89.3 29.0 %fusion.4 = f32[8,9216]{1,0:T(8,128)} fusion(bf16[8,4608]{1,0:T(8,128)(2,1)S(1)} %all_gather.10, bf16[4608,9216]{1,0:T(8,128)(2,1)} %param.2), kind=kOutput, calls=%fused_computation.17 | convolution fusion | flops 679477248 | bytes 85303296 | tf_op jit(solution)/shard_map/dot_general | solution.py:34
  118.3 0.0 reduce-scatter.6.cloned.1.call-update
  118.3 0.0 reduce-scatter.8.cloned.1.call-start
  118.4 31.0 %reduce-scatter.6.cloned.1.call-done = f32[8,1152]{1,0:T(8,128)} async-done(((f32[8,9216]{1,0:T(8,128)}), f32[8,1152]{1,0:T(8,128)}) %reduce-scatter.6.cloned.1.call-update) | async-done | bytes 36880 | tf_op jit(solution)/shard_map/reduce_scatter | solution.py:15
  149.3 0.0 copy-done.1
  149.3 0.9 fusion
  150.3 14.0 %all_gather.11 = bf16[8,9216]{1,0:T(8,128)(2,1)S(1)} all-gather(bf16[8,1152]{1,0:T(8,128)(2,1)S(1)} %get-tuple-element.10), channel_id=1, replica_groups=mesh['row'=8,'col'=4] {'row'}, dimensions={1}, use_global_device_ids=true | all-gather | bytes 165888 | tf_op jit(solution)/shard_map/all_gather | solution.py:27
  164.3 31.8 %fusion.5 = f32[8,4608]{1,0:T(8,128)} fusion(bf16[8,9216]{1,0:T(8,128)(2,1)S(1)} %all_gather.11, bf16[4608,9216]{1,0:T(8,128)(2,1)} %param.2), kind=kOutput, calls=%fused_computation.18 | convolution fusion | flops 679477248 | bytes 85229568 | tf_op jit(solution)/shard_map/dot_general | solution.py:22
  196.0 0.0 reduce-scatter.8.cloned.1.call-update
  196.1 22.0 %reduce-scatter.8.cloned.1.call-done = f32[8,1152]{1,0:T(8,128)} async-done(((f32[8,4608]{1,0:T(8,128)}), f32[8,1152]{1,0:T(8,128)}) %reduce-scatter.8.cloned.1.call-update) | async-done | bytes 36880 | tf_op jit(solution)/shard_map/reduce_scatter | solution.py:11
  218.1 0.0 copy-done
  218.1 1.5 multiply_reduce_fusion
  219.6 39.3 %all-reduce = (f32[8,1]{0,1:T(1,128)S(1)}, f32[8,1]{0,1:T(1,128)S(1)}, f32[8,1]{0,1:T(1,128)S(1)}, f32[8]{0:T(128)S(1)}) all-reduce(f32[8,1]{0,1:T(1,128)S(1)} %get-tuple-element.12, f32[8,1]{0,1:T(1,128)S(1)} %multiply_bitcast_fusion.1, f32[8,1]{0,1:T(1,128)S(1)} %get-tuple-element.13, ...), channel_id=1, replica_groups=mesh['row'=8,'col'=4] {'row','col'}, use_global_device_ids=true, to_apply=%region_10.0 | all-reduce | flops 32 | bytes 256 | tf_op jit(solution)/shard_map/psum | solution.py:41
  259.0 0.6 pad_maximum_fusion
  (4 shorter events, 0.0 us)
Async XLA Ops:
  7.2 73.1 %reduce-scatter.4.cloned.1.call-start = ((), (), s32[]{:S(2)}) async-start(), calls=%async_computation.3 | async-start | bytes 184320 | tf_op jit(solution)/shard_map/reduce_scatter | solution.py:11
  23.7 125.6 %copy-start.1 = (f32[8,1,1152]{2,1,0:T(1,128)S(1)}, f32[8,1,1152]{2,1,0:T(1,128)}, u32[]{:S(2)}) copy-start(f32[8,1,1152]{2,1,0:T(1,128)} %param.3) | copy-start | bytes 110596
  55.5 93.8 %reduce-scatter.6.cloned.1.call-start = ((), (), s32[]{:S(2)}) async-start(), calls=%async_computation.4 | async-start | bytes 331776 | tf_op jit(solution)/shard_map/reduce_scatter | solution.py:15
  89.3 128.8 %copy-start = (f32[8,1152]{1,0:T(8,128)S(1)}, f32[8,1152]{1,0:T(8,128)}, u32[]{:S(2)}) copy-start(f32[8,1152]{1,0:T(8,128)} %reduce-scatter.4.cloned.1.call-done) | copy-start | bytes 110596
  118.3 99.8 %reduce-scatter.8.cloned.1.call-start = ((), (), s32[]{:S(2)}) async-start(), calls=%async_computation.5 | async-start | bytes 184320 | tf_op jit(solution)/shard_map/reduce_scatter | solution.py:11
Sparse Core Ops, SparseCore 0:
  55.6 24.5 reduce-scatter.3
  118.4 30.8 reduce-scatter.5
  196.2 21.8 reduce-scatter.7
where the time goes:
time: 267 us; the launch traced here: 266 us
  matrix products  92.5 us (35%)
  waiting for transfers between devices  77.7 us (29%)
  blocking collectives  77.3 us (29%)
  between operations  13.8 us (5%)
  other arithmetic  3.83 us (1%)
    dot_general x2, matrix products, accumulate(): lax.dot_general(portion, hamiltonian, (((1,), (1,)), ((), ())), preferred...  63.5 us
    reduce_scatter x2, waiting for transfers between devices, reduce_cols(): return lax.psum_scatter(product, 'col', scatter_dimension=1, tiled=True)  46.7 us
    psum x1, blocking collectives, reduce_each(): return lax.psum(partial_sq, ('row', 'col'))  39.3 us
    reduce_scatter x1, waiting for transfers between devices, reduce_rows(): return lax.psum_scatter(product, 'row', scatter_dimension=1, tiled=True)  31 us
    all_gather x2, blocking collectives, from_columns(): lax.all_gather(narrow, 'row', axis=1, tiled=True)  29.7 us
    dot_general x1, matrix products, accumulate(): return jnp.dot(portion, hamiltonian, preferred_element_type=jnp.float32)  29 us
    all_gather x1, blocking collectives, from_rows(): lax.all_gather(narrow, 'col', axis=1, tiled=True)  8.24 us
  transfers between devices with their start and end apart: 3, of which 3 were waited for; matrix products, arithmetic and copies ran while one was open for 0% of the time, Pallas kernels for 0%

commit v1 on v0

--- a/solution.py
+++ b/solution.py
@@ -24,7 +24,13 @@
         )
 
     empty = jnp.zeros((vec_count, hamiltonian.shape[0]), jnp.float32)
-    return accumulate(empty, lax.all_gather(narrow, "row", axis=1, tiled=True), jnp.int32(0))
+    return accumulate(
+        empty,
+        jnp.concatenate(
+            lax.all_to_all(jnp.stack([narrow] * lax.axis_size("row")), "row", 0, 0), axis=1
+        ),
+        jnp.int32(0),
+    )
 
 
 def from_rows(narrow, hamiltonian):

time: 267 us -> 259 us (0.970)
  blocking collectives: 77.3 us -> 70.1 us
    all_gather x2 -> x0, blocking collectives: 29.7 us -> none  [from_columns(): lax.all_gather(narrow, 'row', axis=1, tiled=True)]
    all_to_all x0 -> x2, blocking collectives: none -> 22.5 us  [from_columns(): lax.all_to_all(jnp.stack([narrow] * lax.axis_size('row')), 'row', 0, 0)]
where the time goes in v1:
time: 259 us; the launch traced here: 258 us
  matrix products  92.5 us (36%)
  waiting for transfers between devices  77 us (30%)
  blocking collectives  70.1 us (27%)
  between operations  13.8 us (5%)
  other arithmetic  3.83 us (1%)
    dot_general x2, matrix products, accumulate(): lax.dot_general(portion, hamiltonian, (((1,), (1,)), ((), ())), preferred...  63.5 us
    reduce_scatter x2, waiting for transfers between devices, reduce_cols(): return lax.psum_scatter(product, 'col', scatter_dimension=1, tiled=True)  46 us
    psum x1, blocking collectives, reduce_each(): return lax.psum(partial_sq, ('row', 'col'))  39.3 us
    reduce_scatter x1, waiting for transfers between devices, reduce_rows(): return lax.psum_scatter(product, 'row', scatter_dimension=1, tiled=True)  30.9 us
    dot_general x1, matrix products, accumulate(): return jnp.dot(portion, hamiltonian, preferred_element_type=jnp.float32)  29 us
    all_to_all x2, blocking collectives, from_columns(): lax.all_to_all(jnp.stack([narrow] * lax.axis_size('row')), 'row', 0, 0)  22.5 us
    all_gather x1, blocking collectives, from_rows(): lax.all_gather(narrow, 'col', axis=1, tiled=True)  8.26 us
  transfers between devices with their start and end apart: 3, of which 3 were waited for; matrix products, arithmetic and copies ran while one was open for 0% of the time, Pallas kernels for 0%

profile of v1, /device:TPU:0, one launch (start us, length us, event | category | flops | bytes accessed | tf_op | source)
XLA Modules:
  0.0 258.1 jit_solution(14730327101020975513)
XLA Ops:
  7.2 0.0 reduce-scatter.4.cloned.1.call-start
  7.2 0.8 copy.12
  8.0 13.1 %all_to_all.10 = bf16[8,8,1152]{2,1,0:T(8,128)(2,1)S(1)} all-to-all(bf16[8,8,1152]{2,1,0:T(8,128)(2,1)S(1)} %stack.14), channel_id=1, replica_groups=mesh['row'=8,'col'=4] {'row'}, dimensions={0} | all-to-all | bytes 294912 | tf_op jit(solution)/shard_map/all_to_all | solution.py:30
  21.1 0.0 copy-start.1
  21.1 31.8 %fusion.3 = f32[8,4608]{1,0:T(8,128)} fusion(bf16[8,9216]{1,0:T(8,128)(2,1)S(1)} %bitcast.30, bf16[4608,9216]{1,0:T(8,128)(2,1)} %param.2), kind=kOutput, calls=%fused_computation.16 | convolution fusion | flops 679477248 | bytes 85229568 | tf_op jit(solution)/shard_map/dot_general | solution.py:22
  52.9 0.0 reduce-scatter.4.cloned.1.call-update
  52.9 0.0 reduce-scatter.6.cloned.1.call-start
  53.0 22.9 %reduce-scatter.4.cloned.1.call-done = f32[8,1152]{1,0:T(8,128)} async-done(((f32[8,4608]{1,0:T(8,128)}), f32[8,1152]{1,0:T(8,128)}) %reduce-scatter.4.cloned.1.call-update) | async-done | bytes 36880 | tf_op jit(solution)/shard_map/reduce_scatter | solution.py:11
  75.9 0.8 convert_element_type.12
  76.7 8.3 %all_gather.3 = bf16[8,4608]{1,0:T(8,128)(2,1)S(1)} all-gather(bf16[8,1152]{1,0:T(8,128)(2,1)S(1)} %convert_element_type.12), channel_id=1, replica_groups=mesh['row'=8,'col'=4] {'col'}, dimensions={1}, use_global_device_ids=true | all-gather | bytes 92160 | tf_op jit(solution)/shard_map/all_gather | solution.py:43
  84.9 0.0 copy-start
  84.9 29.0 %fusion.4 = f32[8,9216]{1,0:T(8,128)} fusion(bf16[8,4608]{1,0:T(8,128)(2,1)S(1)} %all_gather.3, bf16[4608,9216]{1,0:T(8,128)(2,1)} %param.2), kind=kOutput, calls=%fused_computation.17 | convolution fusion | flops 679477248 | bytes 85303296 | tf_op jit(solution)/shard_map/dot_general | solution.py:40
  113.9 0.0 reduce-scatter.6.cloned.1.call-update
  114.0 0.0 reduce-scatter.8.cloned.1.call-start
  114.0 30.9 %reduce-scatter.6.cloned.1.call-done = f32[8,1152]{1,0:T(8,128)} async-done(((f32[8,9216]{1,0:T(8,128)}), f32[8,1152]{1,0:T(8,128)}) %reduce-scatter.6.cloned.1.call-update) | async-done | bytes 36880 | tf_op jit(solution)/shard_map/reduce_scatter | solution.py:15
  144.9 0.0 copy-done.1
  144.9 0.9 fusion
  145.9 9.4 %all_to_all.11 = bf16[8,8,1152]{2,1,0:T(8,128)(2,1)S(1)} all-to-all(bf16[8,8,1152]{2,1,0:T(8,128)(2,1)S(1)} %stack.15), channel_id=1, replica_groups=mesh['row'=8,'col'=4] {'row'}, dimensions={0} | all-to-all | bytes 294912 | tf_op jit(solution)/shard_map/all_to_all | solution.py:30
  155.2 31.8 %fusion.5 = f32[8,4608]{1,0:T(8,128)} fusion(bf16[8,9216]{1,0:T(8,128)(2,1)S(1)} %bitcast.31, bf16[4608,9216]{1,0:T(8,128)(2,1)} %param.2), kind=kOutput, calls=%fused_computation.18 | convolution fusion | flops 679477248 | bytes 85229568 | tf_op jit(solution)/shard_map/dot_general | solution.py:22
  187.0 0.0 reduce-scatter.8.cloned.1.call-update
  187.1 23.1 %reduce-scatter.8.cloned.1.call-done = f32[8,1152]{1,0:T(8,128)} async-done(((f32[8,4608]{1,0:T(8,128)}), f32[8,1152]{1,0:T(8,128)}) %reduce-scatter.8.cloned.1.call-update) | async-done | bytes 36880 | tf_op jit(solution)/shard_map/reduce_scatter | solution.py:11
  210.1 0.0 copy-done
  210.1 1.5 multiply_reduce_fusion
  211.7 39.3 %all-reduce = (f32[8,1]{0,1:T(1,128)S(1)}, f32[8,1]{0,1:T(1,128)S(1)}, f32[8,1]{0,1:T(1,128)S(1)}, f32[8]{0:T(128)S(1)}) all-reduce(f32[8,1]{0,1:T(1,128)S(1)} %get-tuple-element.12, f32[8,1]{0,1:T(1,128)S(1)} %multiply_bitcast_fusion.1, f32[8,1]{0,1:T(1,128)S(1)} %get-tuple-element.13, ...), channel_id=1, replica_groups=mesh['row'=8,'col'=4] {'row','col'}, use_global_device_ids=true, to_apply=%region_10.0 | all-reduce | flops 32 | bytes 256 | tf_op jit(solution)/shard_map/psum | solution.py:47
  251.0 0.6 pad_maximum_fusion
  (6 shorter events, 0.1 us)
Async XLA Ops:
  7.2 68.7 %reduce-scatter.4.cloned.1.call-start = ((), (), s32[]{:S(2)}) async-start(), calls=%async_computation.5 | async-start | bytes 184320 | tf_op jit(solution)/shard_map/reduce_scatter | solution.py:11
  21.1 123.8 %copy-start.1 = (f32[8,1,1152]{2,1,0:T(1,128)S(1)}, f32[8,1,1152]{2,1,0:T(1,128)}, u32[]{:S(2)}) copy-start(f32[8,1,1152]{2,1,0:T(1,128)} %param.3) | copy-start | bytes 110596
  52.9 92.0 %reduce-scatter.6.cloned.1.call-start = ((), (), s32[]{:S(2)}) async-start(), calls=%async_computation.6 | async-start | bytes 331776 | tf_op jit(solution)/shard_map/reduce_scatter | solution.py:15
  84.9 125.2 %copy-start = (f32[8,1152]{1,0:T(8,128)S(1)}, f32[8,1152]{1,0:T(8,128)}, u32[]{:S(2)}) copy-start(f32[8,1152]{1,0:T(8,128)} %reduce-scatter.4.cloned.1.call-done) | copy-start | bytes 110596
  114.0 96.2 %reduce-scatter.8.cloned.1.call-start = ((), (), s32[]{:S(2)}) async-start(), calls=%async_computation.7 | async-start | bytes 184320 | tf_op jit(solution)/shard_map/reduce_scatter | solution.py:11
Sparse Core Ops, SparseCore 0:
  53.0 22.8 reduce-scatter.3
  114.1 30.8 reduce-scatter.5
  187.2 22.9 reduce-scatter.7
